TPU v7x, 32 devices: a whole 2x2x4 slice. The times are simulated.
32 devices in a mesh: tables: 8 (over z, y), cells: 4 (over x, core).
Axes of the slice: x: 2, y: 2, z: 4, core: 2. Of those that a mesh axis runs over, the one named last changes fastest.
Arguments:
- cells_in: bfloat16 [8, 128, 112, 192], P('tables', 'cells'), may hold values from -6 to 6
- train_count: int32 [8], P('tables'), may hold values from 32 to 96
- feat_count: int32 [8], P('tables'), may hold values from 28 to 112
- feat_qkv: bfloat16 [192, 576], replicated, may hold values from -2 to 2
- feat_proj: bfloat16 [192, 192], replicated, may hold values from -2 to 2
- row_qkv: bfloat16 [192, 576], replicated, may hold values from -2 to 2
- row_proj: bfloat16 [192, 192], replicated, may hold values from -0.4375 to 0.4375
- w_in: bfloat16 [192, 768], replicated, may hold values from -0.4375 to 0.4375
- w_out: bfloat16 [768, 192], replicated, may hold values from -0.21875 to 0.21875
- cotangent: bfloat16 [8, 128, 112, 192], P('tables', 'cells'), may hold values from -6 to 6
Outputs:
- cells_out: bfloat16 [8, 128, 112, 192], P('tables', 'cells')
- grad_in: float32 [192, 768], P(None, ('tables', 'cells'))
- grad_out: float32 [768, 192], P(('tables', 'cells'))
All inputs are finite; a program needn't handle non-finite values.
Results may differ from a plain program's by a relative error of at most 0.018.
Values may be sent and summed in bfloat16 or wider, within the bound.
A program may use at most 128 MiB of HBM per device.

v0:
```python
import math

import jax
import jax.numpy as jnp
from jax import lax
from jax.sharding import PartitionSpec as P

HEADS = 6
HEAD_DIM = 32


def layer_norm(values):
    mean = jnp.mean(values, axis=-1, keepdims=True)
    centred = values - mean
    var = jnp.mean(centred * centred, axis=-1, keepdims=True)
    return centred / jnp.sqrt(var + 1e-05)


def feature_layer(block, feat_limit, weight_qkv, weight_proj):
    rows, feats, width = block.shape
    packed = jnp.dot(
        block.reshape(rows * feats, width), weight_qkv, preferred_element_type=jnp.float32
    )
    packed = packed.astype(jnp.bfloat16).reshape(rows, feats, 3, HEADS, HEAD_DIM)
    query, keys, values = (packed[:, :, 0], packed[:, :, 1], packed[:, :, 2])
    score = jnp.einsum(
        "rfhd,rghd->rhfg", query, keys, preferred_element_type=jnp.float32
    ) / jnp.sqrt(jnp.float32(HEAD_DIM))
    keep = jnp.arange(feats, dtype=jnp.int32) < feat_limit
    score = jnp.where(keep[None, None, None, :], score, jnp.float32(-1e30))
    probs = jax.nn.softmax(score, axis=-1).astype(jnp.bfloat16)
    attended = jnp.einsum(
        "rhfg,rghd->rfhd", probs, values, preferred_element_type=jnp.float32
    ).astype(jnp.bfloat16)
    mixed = jnp.dot(
        attended.reshape(rows * feats, width), weight_proj, preferred_element_type=jnp.float32
    )
    total = block.reshape(rows * feats, width).astype(jnp.float32) + mixed
    return layer_norm(total).astype(jnp.bfloat16).reshape(rows, feats, width)


def row_single(column, train_limit, weight_qkv, weight_proj):
    rows, width = column.shape
    packed = jnp.dot(column, weight_qkv, preferred_element_type=jnp.float32)
    packed = packed.astype(jnp.bfloat16).reshape(rows, 3, HEADS, HEAD_DIM)
    query, keys, values = (packed[:, 0], packed[:, 1], packed[:, 2])
    score = jnp.einsum("ihd,jhd->hij", query, keys, preferred_element_type=jnp.float32) / jnp.sqrt(
        jnp.float32(HEAD_DIM)
    )
    keep = jnp.arange(rows, dtype=jnp.int32) < train_limit
    score = jnp.where(keep[None, None, :], score, jnp.float32(-1e30))
    probs = jax.nn.softmax(score, axis=-1).astype(jnp.bfloat16)
    attended = jnp.einsum("hij,jhd->ihd", probs, values, preferred_element_type=jnp.float32)
    attended = attended.astype(jnp.bfloat16).reshape(rows, width)
    mixed = jnp.dot(attended, weight_proj, preferred_element_type=jnp.float32)
    return layer_norm(column.astype(jnp.float32) + mixed).astype(jnp.bfloat16)


def exact_gelu(values):
    return jax.nn.gelu(values, approximate=False)


def dense_block(normed_cells, cot_cells, w_in, w_out):
    shape = normed_cells.shape
    normed = normed_cells.reshape(-1, shape[-1])
    cot_flat = cot_cells.reshape(-1, shape[-1])
    pre = jnp.dot(normed, w_in, preferred_element_type=jnp.float32)
    act_f, backward = jax.vjp(exact_gelu, pre)
    act = act_f.astype(jnp.bfloat16)
    output = (
        normed.astype(jnp.float32) + jnp.dot(act, w_out, preferred_element_type=jnp.float32)
    ).astype(jnp.bfloat16)
    contract = (((0,), (0,)), ((), ()))
    part_out = lax.dot_general(act, cot_flat, contract, preferred_element_type=jnp.float32)
    dact = lax.dot_general(
        cot_flat, w_out, (((1,), (1,)), ((), ())), preferred_element_type=jnp.float32
    )
    dpre = backward(dact)[0].astype(jnp.bfloat16)
    part_in = lax.dot_general(normed, dpre, contract, preferred_element_type=jnp.float32)
    return (output.reshape(shape), part_in, part_out)


def per_device(
    cells_in,
    train_count,
    feat_count,
    feat_qkv,
    feat_proj,
    row_qkv,
    row_proj,
    w_in,
    w_out,
    cotangent,
):
    block = cells_in[0]
    train_limit = train_count[0]
    feat_limit = feat_count[0]
    groups = lax.axis_size("cells")
    mid = feature_layer(block, feat_limit, feat_qkv, feat_proj)
    local_rows, feats, width = mid.shape
    grouped = mid.reshape(local_rows, groups, feats // groups, width)
    columns = jnp.moveaxis(
        lax.all_to_all(grouped, "cells", split_axis=1, concat_axis=0, tiled=True)[:, 0], 1, 0
    )
    done = lax.map(lambda column: row_single(column, train_limit, row_qkv, row_proj), columns)
    exchanged = jnp.moveaxis(done, 0, 1)[:, None]
    normed_cols = exchanged.reshape(local_rows * groups, feats // groups, width)
    normed = lax.all_to_all(normed_cols, "cells", split_axis=0, concat_axis=1, tiled=True)
    output, part_in, part_out = dense_block(normed, cotangent[0], w_in, w_out)
    whole_rows = block.shape[0] * groups
    factor = 1.0 / math.sqrt(lax.axis_size("tables") * whole_rows * block.shape[1])
    part_in = part_in * factor
    part_out = part_out * factor
    table_in, table_out = (
        lax.psum_scatter(
            part_in.astype(jnp.bfloat16), "tables", scatter_dimension=1, tiled=True
        ).astype(jnp.float32),
        lax.psum_scatter(
            part_out.astype(jnp.bfloat16), "tables", scatter_dimension=0, tiled=True
        ).astype(jnp.float32),
    )
    grad_in, grad_out = (
        lax.psum_scatter(
            table_in.astype(jnp.bfloat16), "cells", scatter_dimension=1, tiled=True
        ).astype(jnp.float32),
        lax.psum_scatter(
            table_out.astype(jnp.bfloat16), "cells", scatter_dimension=0, tiled=True
        ).astype(jnp.float32),
    )
    return (output[None], grad_in, grad_out)


def solution(mesh):
    return jax.shard_map(
        per_device,
        mesh=mesh,
        in_specs=(
            P("tables", "cells", None, None),
            P("tables"),
            P("tables"),
            P(),
            P(),
            P(),
            P(),
            P(),
            P(),
            P("tables", "cells", None, None),
        ),
        out_specs=(
            P("tables", "cells", None, None),
            P(None, ("tables", "cells")),
            P(("tables", "cells"), None),
        ),
        check_vma=False,
    )
```

profile of v0, /device:TPU:0, one launch (start us, length us, event | category | flops | bytes accessed | tf_op | source)
XLA Modules:
  0.0 452.7 jit_solution(6171762001614699345)
XLA Ops:
  7.2 2.5 copy.40
  9.7 3.1 reshape_squeeze.7
  12.8 4.2 convolution_convert_fusion.2
  17.0 9.7 %reshape.59 = bf16[32,112,3,6,32]{1,0,4,3,2:T(8,128)(2,1)} reshape(bf16[3584,576]{0,1:T(8,128)(2,1)} %convolution_convert_fusion.2) | data formatting | bytes 8257536 | tf_op jit(solution)/shard_map/reshape | solution.py:24
  26.7 3.2 fusion.38
  30.5 17.4 %fusion.25 = f32[32,6,112,112]{2,3,1,0:T(8,128)} fusion(bf16[32,112,1,6,32]{1,0,4,3,2:T(8,128)(2,1)S(1)} %get-tuple-element.75, bf16[32,112,1,6,32]{1,0,4,3,2:T(8,128)(2,1)S(1)} %get-tuple-element.74), kind=kOutput, calls=%fused_computation.59 | convolution fusion | flops 154140672 | bytes 12386304 | tf_op jit(solution)/shard_map/rfhd,rghd->rhfg/dot_general | solution.py:26
  47.9 15.7 %fusion.39 = (f32[32,6,112]{2,1,0:T(8,128)S(1)}, f32[32,6,112,112]{2,3,1,0:T(8,128)}) fusion(f32[32,6,112,112]{2,3,1,0:T(8,128)} %fusion.25, pred[112]{0:T(512)(128)(4,1)S(1)} %iota_compare_fusion.1), kind=kOutput, calls=%fused_computation.78 | output fusion | flops 14450799 | bytes 19353712 | tf_op jit(solution)/shard_map/sub | solution.py:31
  63.6 6.6 %fusion.26 = bf16[32,112,6,32]{1,3,2,0:T(8,128)(2,1)S(1)} fusion(f32[32,6,112,112]{2,3,1,0:T(8,128)} %get-tuple-element.77, f32[32,6,112]{2,1,0:T(8,128)S(1)} %get-tuple-element.76, bf16[32,112,1,6,32]{1,0,4,3,2:T(8,128)(2,1)S(1)} %get-tuple-element.73), kind=kOutput, calls=%fused_computation.62 | convolution fusion | flops 159645696 | bytes 12472320 | tf_op jit(solution)/shard_map/rhfg,rghd->rfhd/dot_general | solution.py:32
  70.2 1.0 copy.45
  71.2 4.0 reshape.60
  75.2 1.9 fusion.40
  77.8 2.3 copy.46
  80.1 2.7 reshape_reshape.3
  82.8 2.3 copy.47
  85.1 4.2 all-to-all-start
  89.4 22.9 %all-to-all-done = bf16[32,4,28,192]{3,0,2,1:T(8,128)(2,1)S(1)} async-done(((bf16[32,4,28,192]{3,0,2,1:T(8,128)(2,1)}), bf16[32,4,28,192]{3,0,2,1:T(8,128)(2,1)S(1)}, u32[]{:S(2)}, u32[]{:S(2)}) %all-to-all-start) | async-done | bytes 1376288 | tf_op jit(solution)/shard_map/all_to_all | solution.py:103
  112.2 1.5 copy.48
  113.7 3.1 copy.49
  116.8 77.2 %while.10 = (s32[]{:T(128)}, bf16[28,128,192]{1,2,0:T(8,128)(2,1)}, bf16[28,128,192]{1,2,0:T(8,128)(2,1)S(1)}, bf16[192,576]{1,0:T(8,128)(2,1)S(1)}, s32[]{:T(128)}, /*index=5*/bf16[192,192]{1,0:T(8,128)(2,1)S(1)}, s32[]{:T(128)}) while((s32[]{:T(128)}, bf16[28,128,192]{1,2,0:T(8,128)(2,1)}, bf16[28,128,192]{1,2,0:T(8,128)(2,1)S(1)}, ...), condition=%wide.region_9.10_spmd, body=%wide.region_4.9_spmd.sunk | while | flops 57828608 | bytes 2446553 | solution.py:105
  117.1 0.7 iota_compare_fusion.3
  119.8 0.7 iota_compare_fusion.3
  122.6 0.7 iota_compare_fusion.3
  125.3 0.7 iota_compare_fusion.3
  128.1 0.7 iota_compare_fusion.3
  130.9 0.7 iota_compare_fusion.3
  133.6 0.7 iota_compare_fusion.3
  136.4 0.7 iota_compare_fusion.3
  139.1 0.7 iota_compare_fusion.3
  141.9 0.7 iota_compare_fusion.3
  144.7 0.7 iota_compare_fusion.3
  147.4 0.7 iota_compare_fusion.3
  150.2 0.7 iota_compare_fusion.3
  152.9 0.7 iota_compare_fusion.3
  155.7 0.7 iota_compare_fusion.3
  158.4 0.7 iota_compare_fusion.3
  161.2 0.7 iota_compare_fusion.3
  164.0 0.7 iota_compare_fusion.3
  166.7 0.7 iota_compare_fusion.3
  169.5 0.7 iota_compare_fusion.3
  172.2 0.7 iota_compare_fusion.3
  175.0 0.7 iota_compare_fusion.3
  186.0 0.7 iota_compare_fusion.3
  194.0 4.5 copy.50
  198.5 3.6 all-to-all-start.1
  202.1 3.6 copy.54
  205.7 4.4 reshape_squeeze.8
  210.1 17.6 %all-to-all-done.1 = bf16[128,28,192]{2,1,0:T(8,128)(2,1)S(1)} async-done(((bf16[128,28,192]{2,1,0:T(8,128)(2,1)}), bf16[128,28,192]{2,1,0:T(8,128)(2,1)S(1)}, u32[]{:S(2)}, u32[]{:S(2)}) %all-to-all-start.1) | async-done | bytes 1376288 | tf_op jit(solution)/shard_map/all_to_all | solution.py:108
  227.7 1.6 copy.52
  229.3 2.8 reshape.61
  232.1 27.4 %multiply_convert_fusion = (bf16[3584,768]{1,0:T(8,128)(2,1)}, f32[3584,768]{1,0:T(8,128)}, f32[3584,768]{1,0:T(8,128)}) fusion(bf16[3584,192]{1,0:T(8,128)(2,1)S(1)} %reshape.61, bf16[192,768]{1,0:T(8,128)(2,1)S(1)} %copy-done), kind=kOutput, calls=%fused_computation.28 | convolution fusion | flops 1235877888 | bytes 29196288 | tf_op jit(solution)/shard_map/dot_general | solution.py:67
  259.5 13.1 %fusion.29 = bf16[192,768]{1,0:T(8,128)(2,1)S(1)} fusion(bf16[3584,192]{1,0:T(8,128)(2,1)S(1)} %reshape.61, f32[3584,768]{1,0:T(8,128)} %get-tuple-element.70, f32[3584,768]{1,0:T(8,128)} %get-tuple-element.80, bf16[3584,192]{0,1:T(8,128)(2,1)S(1)} %copy-done.4, bf16[768,192]{0,1:T(8,128)(2,1)} %param.20), kind=kOutput, calls=%fused_computation.66 | convolution fusion | flops 2152759296 | bytes 25362432 | tf_op jit(solution)/shard_map/dot_general | solution.py:79
  272.6 0.9 copy.60
  273.6 5.0 %fusion.27 = bf16[768,192]{1,0:T(8,128)(2,1)} fusion(bf16[3584,768]{1,0:T(8,128)(2,1)} %get-tuple-element.69, bf16[3584,192]{0,1:T(8,128)(2,1)S(1)} %copy-done.4), kind=kOutput, calls=%fused_computation.64 | convolution fusion | flops 1057259520 | bytes 7176192 | tf_op jit(solution)/shard_map/dot_general | solution.py:74
  278.7 58.3 %reduce-scatter.13.cloned.1.call-done = bf16[96,192]{1,0:T(8,128)(2,1)} async-done(((bf16[768,192]{1,0:T(8,128)(2,1)}), bf16[96,192]{1,0:T(8,128)(2,1)}) %reduce-scatter.13.cloned.1.call-update) | async-done | bytes 36880
  337.0 1.6 copy.53
  338.6 62.9 %reduce-scatter.9.cloned.1.call-done = bf16[96,192]{1,0:T(8,128)(2,1)} async-done(((bf16[768,192]{1,0:T(8,128)(2,1)}), bf16[96,192]{1,0:T(8,128)(2,1)}) %reduce-scatter.9.cloned.1.call-update) | async-done | bytes 36880 | tf_op jit(solution)/shard_map/reduce_scatter | solution.py:118
  401.5 5.6 %fusion.22 = bf16[3584,192]{0,1:T(8,128)(2,1)} fusion(bf16[3584,768]{1,0:T(8,128)(2,1)} %get-tuple-element.69, bf16[768,192]{0,1:T(8,128)(2,1)} %param.20, bf16[3584,192]{0,1:T(8,128)(2,1)S(1)} %copy.53), kind=kOutput, calls=%fused_computation.53 | convolution fusion | flops 1059028992 | bytes 8552448 | tf_op jit(solution)/shard_map/dot_general | solution.py:71
  407.1 3.4 broadcast_in_dim_reshape.3
  410.5 1.8 copy.55
  412.3 10.3 %reduce-scatter.15.cloned.1.call-done = bf16[24,192]{1,0:T(8,128)(2,1)} async-done(((bf16[96,192]{1,0:T(8,128)(2,1)}), bf16[24,192]{1,0:T(8,128)(2,1)}) %reduce-scatter.15.cloned.1.call-update) | async-done | bytes 9232
  422.6 0.8 copy.63
  423.4 0.7 copy.56
  424.1 20.3 %reduce-scatter.11.cloned.1.call-done = bf16[24,192]{1,0:T(8,128)(2,1)} async-done(((bf16[96,192]{1,0:T(8,128)(2,1)}), bf16[24,192]{1,0:T(8,128)(2,1)}) %reduce-scatter.11.cloned.1.call-update) | async-done | bytes 9232 | tf_op jit(solution)/shard_map/reduce_scatter | solution.py:126
  444.4 1.3 convert_element_type.77
  (283 shorter events, 62.1 us)
Async XLA Ops:
  7.2 224.9 %copy-start = (bf16[192,768]{1,0:T(8,128)(2,1)S(1)}, bf16[192,768]{1,0:T(8,128)(2,1)}, u32[]{:S(2)}) copy-start(bf16[192,768]{1,0:T(8,128)(2,1)} %param.19) | copy-start | bytes 884740
  63.6 11.6 %copy-start.5 = (bf16[192,192]{1,0:T(8,128)(2,1)S(1)}, bf16[192,192]{1,0:T(8,128)(2,1)}, u32[]{:S(2)}) copy-start(bf16[192,192]{1,0:T(8,128)(2,1)} %param.16) | copy-start | bytes 221188
  77.8 39.0 %copy-start.2 = (bf16[192,576]{1,0:T(8,128)(2,1)S(1)}, bf16[192,576]{1,0:T(8,128)(2,1)}, u32[]{:S(2)}) copy-start(bf16[192,576]{1,0:T(8,128)(2,1)} %param.17) | copy-start | bytes 663556
  77.8 39.0 %copy-start.3 = (bf16[192,192]{1,0:T(8,128)(2,1)S(1)}, bf16[192,192]{1,0:T(8,128)(2,1)}, u32[]{:S(2)}) copy-start(bf16[192,192]{1,0:T(8,128)(2,1)} %param.18) | copy-start | bytes 221188
  85.1 27.1 %all-to-all-start = ((bf16[32,4,28,192]{3,0,2,1:T(8,128)(2,1)}), bf16[32,4,28,192]{3,0,2,1:T(8,128)(2,1)S(1)}, u32[]{:S(2)}, u32[]{:S(2)}) async-start(bf16[32,4,28,192]{3,0,2,1:T(8,128)(2,1)} %copy.47), calls=%async_computation | async-start | bytes 3670016 | tf_op jit(solution)/shard_map/all_to_all | solution.py:103
  198.5 29.2 %all-to-all-start.1 = ((bf16[128,28,192]{2,1,0:T(8,128)(2,1)}), bf16[128,28,192]{2,1,0:T(8,128)(2,1)S(1)}, u32[]{:S(2)}, u32[]{:S(2)}) async-start(bf16[128,28,192]{2,1,0:T(8,128)(2,1)} %bitcast.121), calls=%async_computation.1 | async-start | bytes 4194304 | tf_op jit(solution)/shard_map/all_to_all | solution.py:108
  202.1 134.9 %reduce-scatter.13.cloned.1.call-start = ((), (), s32[]{:S(2)}) async-start(), calls=%async_computation.8 | async-start | bytes 442368
  232.1 27.4 %copy-start.4 = (bf16[3584,192]{0,1:T(8,128)(2,1)S(1)}, bf16[3584,192]{0,1:T(8,128)(2,1)}, u32[]{:S(2)}) copy-start(bf16[3584,192]{0,1:T(8,128)(2,1)} %reshape_squeeze.8) | copy-start | bytes 4128772
  273.6 128.0 %reduce-scatter.9.cloned.1.call-start = ((), (), s32[]{:S(2)}) async-start(), calls=%async_computation.6 | async-start | bytes 442368 | tf_op jit(solution)/shard_map/reduce_scatter | solution.py:118
  273.6 172.2 %copy-start.1 = (bf16[192,768]{1,0:T(8,128)(2,1)S(1)}, bf16[192,768]{1,0:T(8,128)(2,1)}, u32[]{:S(2)}) copy-start(bf16[192,768]{1,0:T(8,128)(2,1)} %param.19) | copy-start | bytes 884740
  278.6 144.0 %reduce-scatter.15.cloned.1.call-start = ((), (), s32[]{:S(2)}) async-start(), calls=%async_computation.9 | async-start | bytes 61440
  337.0 107.4 %reduce-scatter.11.cloned.1.call-start = ((), (), s32[]{:S(2)}) async-start(), calls=%async_computation.7 | async-start | bytes 61440 | tf_op jit(solution)/shard_map/reduce_scatter | solution.py:126
Sparse Core Ops, SparseCore 0:
  273.7 63.2 reduce-scatter.12
  340.2 61.2 reduce-scatter.8
  403.9 18.6 reduce-scatter.14
  424.9 19.5 reduce-scatter.10
where the time goes:
time: 454 us; the launch traced here: 453 us
  waiting for transfers between devices  192 us (42%)
  matrix products  119 us (26%)
  local copies, waits for them, and re-layouts  61.3 us (14%)
  other arithmetic  55.7 us (12%)
  between operations  15.1 us (3%)
  starting transfers between devices  8 us (2%)
    unnamed x6, waiting for transfers between devices  68.7 us
    reduce_scatter x1, waiting for transfers between devices, per_device(): lax.psum_scatter(part_out.astype(jnp.bfloat16), 'tables', scatter_dimensi...  62.9 us
    dot_general x1, matrix products, dense_block(): pre = jnp.dot(normed, w_in, preferred_element_type=jnp.float32)  27.4 us
    all_to_all x1, waiting for transfers between devices, per_device(): lax.all_to_all(grouped, 'cells', split_axis=1, concat_axis=0, tiled=True)  22.9 us
    reduce_scatter x1, waiting for transfers between devices, per_device(): lax.psum_scatter(table_out.astype(jnp.bfloat16), 'cells', scatter_dimensi...  20.3 us
    lt x28, other arithmetic, row_single(): keep = jnp.arange(rows, dtype=jnp.int32) < train_limit  18.3 us
    dynamic_update_slice x28, other arithmetic, per_device(): lax.map(lambda column: row_single(column, train_limit, row_qkv, row_proj)...  18.2 us
    all_to_all x1, waiting for transfers between devices, per_device(): lax.all_to_all(normed_cols, 'cells', split_axis=0, concat_axis=1, tiled=T...  17.6 us
  transfers between devices with their start and end apart: 6, of which 6 were waited for; matrix products, arithmetic and copies ran while one was open for 6% of the time, Pallas kernels for 0%

commit v1 on v0

v1 whole, which is shorter than its diff:
```python
import math

import jax
import jax.numpy as jnp
from jax import lax
from jax.experimental import pallas as pl
from jax.experimental.pallas import tpu as pltpu
from jax.sharding import PartitionSpec as P

HEADS = 6
HEAD_DIM = 32
NEG = -1e30
LOG2E = math.log2(math.e)
SCALE = LOG2E / math.sqrt(HEAD_DIM)
AXES = ("tables", "cells")
F32 = jnp.float32
BF16 = jnp.bfloat16


def dot(a, b, ca, cb):
    return lax.dot_general(a, b, (((ca,), (cb,)), ((), ())), preferred_element_type=F32)


def layer_norm(values):
    mean = jnp.mean(values, axis=-1, keepdims=True)
    centred = values - mean
    var = jnp.mean(centred * centred, axis=-1, keepdims=True)
    return centred * lax.rsqrt(var + 1e-05)


def attend(x, w_t, w_proj, limit):
    n, width = x.shape
    packed = dot(w_t, x, 1, 1).astype(BF16)
    keep = lax.broadcasted_iota(jnp.int32, (n, 1), 0) < limit
    step = n if n <= 128 else 128
    heads = []
    for h in range(HEADS):
        lo = h * HEAD_DIM
        keys = packed[width + lo : width + lo + HEAD_DIM]
        vals = packed[2 * width + lo : 2 * width + lo + HEAD_DIM]
        cols = []
        for q0 in range(0, n, step):
            query = packed[lo : lo + HEAD_DIM, q0 : q0 + step]
            score = jnp.where(keep, dot(keys, query, 0, 0), NEG)
            top = jnp.max(score, axis=0, keepdims=True)
            prob = jnp.exp2((score - top) * SCALE)
            total = jnp.sum(prob, axis=0, keepdims=True)
            out = dot(vals, prob.astype(BF16), 1, 0)
            cols.append((out / total).astype(BF16))
        heads.append(cols[0] if len(cols) == 1 else jnp.concatenate(cols, axis=1))
    attended = jnp.concatenate(heads, axis=0)
    return layer_norm(x.astype(F32) + dot(attended, w_proj, 0, 0))


def feature_kernel(limit_ref, x_ref, w_ref, p_ref, o_ref, lo_ref, hi_ref):
    rows, feats, width = x_ref.shape
    limit = limit_ref[0]

    def body(r, carry):
        y = attend(x_ref[r], w_ref[...], p_ref[...], limit)
        spot = pl.ds(r, feats, stride=rows)
        lo_ref[spot, :] = y[:, :128]
        hi_ref[spot, :] = jnp.concatenate([y[:, 128:], jnp.zeros((feats, 256 - width), F32)], axis=1)
        return carry

    lax.fori_loop(0, rows, body, 0)
    o_ref[:, :, :128] = lo_ref[...].reshape(feats, rows, 128).astype(BF16)
    o_ref[:, :, 128:] = hi_ref[...].reshape(feats, rows, 128)[:, :, : width - 128].astype(BF16)


def row_kernel(limit_ref, x_ref, w_ref, p_ref, o_ref):
    groups, block, rows, width = x_ref.shape
    limit = limit_ref[0]

    def body(f, carry):
        x = x_ref[:, f].reshape(groups * rows, width)
        y = attend(x, w_ref[...], p_ref[...], limit)
        o_ref[:, f] = y.astype(BF16).reshape(groups, rows, width)
        return carry

    lax.fori_loop(0, block, body, 0)


def gelu_pair(x):
    bell = jnp.exp2(x * x * (-0.5 * LOG2E))
    t = 1.0 / (1.0 + (0.3275911 * math.sqrt(0.5)) * jnp.abs(x))
    poly = 0.5 * 1.061405429 * t + (0.5 * -1.453152027)
    poly = poly * t + (0.5 * 1.421413741)
    poly = poly * t + (0.5 * -0.284496736)
    poly = poly * t + (0.5 * 0.254829592)
    tail = poly * t * bell
    cdf = jnp.where(x < 0, tail, 1.0 - tail)
    return x * cdf, cdf + x * bell * (1.0 / math.sqrt(2.0 * math.pi))


def dense_kernel(factor, x_ref, c_ref, wi_ref, wo_ref, o_ref, gi_ref, go_ref, lo_ref, hi_ref, ai_ref, ao_ref):
    feats, rows, width = x_ref.shape
    cells = feats * rows
    step = pl.program_id(0)

    @pl.when(step == 0)
    def _():
        ai_ref[...] = jnp.zeros_like(ai_ref)
        ao_ref[...] = jnp.zeros_like(ao_ref)

    lo_ref[...] = x_ref[:, :, :128].astype(F32).reshape(cells, 128)
    hi_ref[:, : width - 128] = x_ref[:, :, 128:].astype(F32).reshape(cells, width - 128)
    group = 8

    def body(i, carry):
        parts = []
        for k in range(group):
            spot = pl.ds(i * group + k, feats, stride=rows)
            parts.append(jnp.concatenate([lo_ref[spot, :], hi_ref[spot, :][:, : width - 128]], axis=1).astype(BF16))
        normed = jnp.concatenate(parts, axis=0)
        here = pl.ds(i * group, group)
        cot = c_ref[here].reshape(group * feats, width)
        pre = dot(normed, wi_ref[...], 1, 0)
        act, slope = gelu_pair(pre)
        act = act.astype(BF16)
        out = normed.astype(F32) + dot(act, wo_ref[...], 1, 0)
        o_ref[here] = out.astype(BF16).reshape(group, feats, width)
        dpre = (dot(cot, wo_ref[...], 1, 1) * slope).astype(BF16)
        ai_ref[...] += dot(normed, dpre, 0, 0)
        ao_ref[...] += dot(cot, act, 0, 0)
        return carry

    lax.fori_loop(0, rows // group, body, 0)

    @pl.when(step == pl.num_programs(0) - 1)
    def _():
        gi_ref[...] = (ai_ref[...] * factor).T.astype(BF16)
        go_ref[...] = (ao_ref[...] * factor).T.astype(BF16)


def whole_spec(array):
    return pl.BlockSpec(array.shape, lambda i: (0,) * array.ndim)


def divisor(n, most):
    return max(k for k in range(1, most + 1) if n % k == 0)


def run_feature(limit, block, w_t, w_proj):
    rows, feats, width = block.shape
    part = 16 if rows % 16 == 0 else rows
    return pl.pallas_call(
        feature_kernel,
        grid=(rows // part,),
        out_shape=jax.ShapeDtypeStruct((feats, rows, width), BF16),
        in_specs=[
            pl.BlockSpec(memory_space=pltpu.SMEM),
            pl.BlockSpec((part, feats, width), lambda i: (i, 0, 0)),
            whole_spec(w_t),
            whole_spec(w_proj),
        ],
        out_specs=pl.BlockSpec((feats, part, width), lambda i: (0, i, 0)),
        scratch_shapes=[pltpu.VMEM((feats * part, 128), F32)] * 2,
        cost_estimate=pl.CostEstimate(flops=4 * 10**9, bytes_accessed=4 * 10**6, transcendentals=0),
        name="feature",
    )(limit, block, w_t, w_proj)


def run_row(limit, columns, w_t, w_proj):
    groups, feats, rows, width = columns.shape
    part = divisor(feats, 4)
    spec = pl.BlockSpec((groups, part, rows, width), lambda i: (0, i, 0, 0))
    return pl.pallas_call(
        row_kernel,
        grid=(feats // part,),
        out_shape=jax.ShapeDtypeStruct(columns.shape, BF16),
        in_specs=[pl.BlockSpec(memory_space=pltpu.SMEM), spec, whole_spec(w_t), whole_spec(w_proj)],
        out_specs=spec,
        cost_estimate=pl.CostEstimate(flops=4 * 10**9, bytes_accessed=4 * 10**6, transcendentals=0),
        name="row",
    )(limit, columns, w_t, w_proj)


def run_dense(factor, normed, cot, w_in, w_out):
    feats, rows, width = normed.shape
    hidden = w_in.shape[1]
    part = 16 if feats % 16 == 0 else feats
    natural = pl.BlockSpec((rows, part, width), lambda i: (0, i, 0))
    grad = pl.BlockSpec((hidden, width), lambda i: (0, 0))
    return pl.pallas_call(
        lambda *refs: dense_kernel(factor, *refs),
        grid=(feats // part,),
        out_shape=[
            jax.ShapeDtypeStruct((rows, feats, width), BF16),
            jax.ShapeDtypeStruct((hidden, width), BF16),
            jax.ShapeDtypeStruct((hidden, width), BF16),
        ],
        in_specs=[
            pl.BlockSpec((part, rows, width), lambda i: (i, 0, 0)),
            natural,
            whole_spec(w_in),
            whole_spec(w_out),
        ],
        out_specs=[natural, grad, grad],
        scratch_shapes=[pltpu.VMEM((part * rows, 128), F32)] * 2 + [pltpu.VMEM((width, hidden), F32)] * 2,
        cost_estimate=pl.CostEstimate(flops=8 * 10**9, bytes_accessed=6 * 10**6, transcendentals=0),
        name="dense",
    )(normed, cot, w_in, w_out)


def per_device(
    cells_in, train_count, feat_count, feat_qkv, feat_proj, row_qkv, row_proj, w_in, w_out, cotangent
):
    block = cells_in[0]
    rows, feats, width = block.shape
    groups = lax.axis_size("cells")
    devices = groups * lax.axis_size("tables")
    mid = run_feature(feat_count, block, feat_qkv.T, feat_proj)
    columns = mid.reshape(groups, feats // groups, rows, width)
    columns = lax.all_to_all(columns, "cells", split_axis=0, concat_axis=0, tiled=True)
    done = run_row(train_count, columns, row_qkv.T, row_proj)
    normed = lax.all_to_all(done, "cells", split_axis=0, concat_axis=0, tiled=True)
    factor = 1.0 / math.sqrt(devices * rows * feats)
    output, part_in, part_out = run_dense(
        factor, normed.reshape(feats, rows, width), cotangent[0], w_in, w_out
    )
    own = part_in.shape[0] // devices
    sends = jnp.concatenate(
        [part_in.reshape(devices, own, width), part_out.reshape(devices, own, width)], axis=1
    )
    got = lax.all_to_all(sends, AXES, split_axis=0, concat_axis=0, tiled=True)
    total = jnp.sum(got.astype(F32), axis=0)
    return output[None], total[:own].T, total[own:]


def solution(mesh):
    return jax.shard_map(
        per_device,
        mesh=mesh,
        in_specs=(
            P("tables", "cells", None, None),
            P("tables"),
            P("tables"),
            P(),
            P(),
            P(),
            P(),
            P(),
            P(),
            P("tables", "cells", None, None),
        ),
        out_specs=(
            P("tables", "cells", None, None),
            P(None, ("tables", "cells")),
            P(("tables", "cells"), None),
        ),
        check_vma=False,
    )
```

time: 454 us -> 233 us (0.51)
  Pallas kernels: 0 us -> 139 us
  waiting for transfers between devices: 192 us -> 57.8 us
  matrix products: 119 us -> 0 us
  other arithmetic: 55.7 us -> 2.41 us
  local copies, waits for them, and re-layouts: 61.3 us -> 16.6 us
  between operations: 15.1 us -> 1.97 us
  starting transfers between devices: 8 us -> 13.8 us
    pallas_call x0 -> x3, Pallas kernels: none -> 139 us  [the longest x1 61.6 us: run_feature(): pl.pallas_call(feature_kernel, grid=(rows // part,), out_shape=jax.ShapeD...]
    dot_general x120 -> x0, matrix products: 110 us -> none  [the longest x1 27.4 us: dense_block(): pre = jnp.dot(normed, w_in, preferred_element_type=jnp.float32)]
    reduce_scatter x2 -> x0, waiting for transfers between devices: 83.2 us -> none  [the longest x1 62.9 us: per_device(): lax.psum_scatter(part_out.astype(jnp.bfloat16), 'tables', scatter_dimensi...]
    unnamed x6 -> x0, waiting for transfers between devices: 68.7 us -> none
    lt x29 -> x0, other arithmetic: 18.3 us -> none  [the longest x28 18.3 us: row_single(): keep = jnp.arange(rows, dtype=jnp.int32) < train_limit]
    dynamic_update_slice x28 -> x0, other arithmetic: 18.2 us -> none  [per_device(): lax.map(lambda column: row_single(column, train_limit, row_qkv, row_proj)...]
    reshape x4 -> x0, local copies, waits for them, and re-layouts: 18 us -> none  [the longest x1 9.68 us: feature_layer(): packed.astype(jnp.bfloat16).reshape(rows, feats, 3, HEADS, HEAD_DIM)]
    all_to_all x2 -> x3, waiting for transfers between devices: 40.5 us -> 57.8 us  [the longest x1 21.3 us: per_device(): lax.all_to_all(columns, 'cells', split_axis=0, concat_axis=0, tiled=True)]
  transfers between devices with their start and end apart: 6 -> 3, of which waited for: 6 -> 3; matrix products, arithmetic and copies ran while one was open for 6% -> 3% of each run, Pallas kernels for 0% -> 0%
where the time goes in v1:
time: 233 us; the launch traced here: 232 us
  Pallas kernels  139 us (60%)
  waiting for transfers between devices  57.8 us (25%)
  local copies, waits for them, and re-layouts  16.6 us (7%)
  starting transfers between devices  13.8 us (6%)
  other arithmetic  2.41 us (1%)
    pallas_call x1, Pallas kernels, run_feature(): pl.pallas_call(feature_kernel, grid=(rows // part,), out_shape=jax.ShapeD...  61.6 us
    pallas_call x1, Pallas kernels, run_row(): pl.pallas_call(row_kernel, grid=(feats // part,), out_shape=jax.ShapeDtyp...  51 us
    pallas_call x1, Pallas kernels, run_dense(): pl.pallas_call(lambda *refs: dense_kernel(factor, *refs), grid=(feats //...  26.9 us
    all_to_all x1, waiting for transfers between devices, per_device(): lax.all_to_all(columns, 'cells', split_axis=0, concat_axis=0, tiled=True)  21.3 us
    all_to_all x1, waiting for transfers between devices, per_device(): lax.all_to_all(done, 'cells', split_axis=0, concat_axis=0, tiled=True)  18.4 us
    all_to_all x1, waiting for transfers between devices, per_device(): got = lax.all_to_all(sends, AXES, split_axis=0, concat_axis=0, tiled=True)  18.1 us
    unnamed x16, local copies, waits for them, and re-layouts  16 us
    all_to_all x1, starting transfers between devices, per_device(): got = lax.all_to_all(sends, AXES, split_axis=0, concat_axis=0, tiled=True)  5.72 us
  transfers between devices with their start and end apart: 3, of which 3 were waited for; matrix products, arithmetic and copies ran while one was open for 3% of the time, Pallas kernels for 0%

profile of v1, /device:TPU:0, one launch (start us, length us, event | category | flops | bytes accessed | tf_op | source)
XLA Modules:
  0.0 232.0 jit_solution(15179434194684849090)
XLA Ops:
  1.3 1.8 copy.14
  3.1 3.8 %copy.13 = bf16[1,32,112,192]{3,2,1,0:T(8,128)(2,1)} copy(bf16[1,32,112,192]{2,3,1,0:T(8,128)(2,1)} %param.10) | data formatting | bytes 2752512 | tf_op args[0]
  6.9 61.6 %feature.1 = bf16[112,32,192]{2,1,0:T(8,128)(2,1)} custom-call(s32[1]{0:T(128)S(6)} %copy.20.limit_ref, bf16[32,112,192]{2,1,0:T(8,128)(2,1)} %bitcast.15, bf16[576,192]{1,0:T(8,128)(2,1)} %bitcast.19, bf16[192,192]{1,0:T(8,128)(2,1)} %p_ref.2), custom_call_target="tpu_custom_call" | custom-call | flops 4000000000 | bytes 4000000 | tf_op jit(solution)/shard_map/feature/pallas_call | solution.py:147
  68.5 0.0 copy-start.4
  68.5 4.4 %all-to-all-start = ((bf16[4,28,32,192]{3,2,1,0:T(8,128)(2,1)}), bf16[4,28,32,192]{3,2,1,0:T(8,128)(2,1)S(1)}, u32[]{:S(2)}, u32[]{:S(2)}) async-start(bf16[4,28,32,192]{3,2,1,0:T(8,128)(2,1)} %bitcast.12), calls=%async_computation | async-start | bytes 3670016 | tf_op jit(solution)/shard_map/all_to_all | solution.py:215
  73.5 0.0 copy-done.4
  73.5 0.9 copy.15
  74.4 21.3 %all-to-all-done.x_ref = bf16[4,28,32,192]{3,2,1,0:T(8,128)(2,1)S(1)} async-done(((bf16[4,28,32,192]{3,2,1,0:T(8,128)(2,1)}), bf16[4,28,32,192]{3,2,1,0:T(8,128)(2,1)S(1)}, u32[]{:S(2)}, u32[]{:S(2)}) %all-to-all-start) | async-done | bytes 1376288 | tf_op jit(solution)/shard_map/all_to_all | solution.py:215
  95.7 0.0 copy-start.1
  95.7 1.3 copy-done.1
  97.0 51.0 %row.1 = bf16[4,28,32,192]{3,2,1,0:T(8,128)(2,1)} custom-call(s32[1]{0:T(128)S(6)} %copy.19.limit_ref, bf16[4,28,32,192]{3,2,1,0:T(8,128)(2,1)} %copy-done.1, bf16[576,192]{1,0:T(8,128)(2,1)} %bitcast.18, bf16[192,192]{1,0:T(8,128)(2,1)} %p_ref.3), custom_call_target="tpu_custom_call" | custom-call | flops 4000000000 | bytes 4000000 | tf_op jit(solution)/shard_map/row/pallas_call | solution.py:168
  148.0 0.0 copy-start.3
  148.0 3.7 %all-to-all-start.1 = ((bf16[4,28,32,192]{3,2,1,0:T(8,128)(2,1)}), bf16[4,28,32,192]{3,2,1,0:T(8,128)(2,1)S(1)}, u32[]{:S(2)}, u32[]{:S(2)}) async-start(bf16[4,28,32,192]{3,2,1,0:T(8,128)(2,1)} %row.1), calls=%async_computation.1 | async-start | bytes 3670016 | tf_op jit(solution)/shard_map/all_to_all | solution.py:217
  151.7 1.9 copy.17.refs_3_
  153.6 0.0 copy-done.3
  153.6 2.5 %copy.16 = bf16[1,32,112,192]{3,2,1,0:T(8,128)(2,1)} copy(bf16[1,32,112,192]{2,3,1,0:T(8,128)(2,1)S(1)} %copy-done.3) | data formatting | bytes 2752512 | tf_op args[9]
  156.1 18.4 %all-to-all-done.1 = bf16[4,28,32,192]{3,2,1,0:T(8,128)(2,1)S(1)} async-done(((bf16[4,28,32,192]{3,2,1,0:T(8,128)(2,1)}), bf16[4,28,32,192]{3,2,1,0:T(8,128)(2,1)S(1)}, u32[]{:S(2)}, u32[]{:S(2)}) %all-to-all-start.1) | async-done | bytes 1376288 | tf_op jit(solution)/shard_map/all_to_all | solution.py:217
  174.5 0.0 copy-start
  174.5 1.3 copy-done
  175.8 26.9 %dense.1 = (bf16[32,112,192]{2,1,0:T(8,128)(2,1)}, bf16[768,192]{1,0:T(8,128)(2,1)}, bf16[768,192]{1,0:T(8,128)(2,1)}) custom-call(bf16[112,32,192]{2,1,0:T(8,128)(2,1)} %bitcast.11, bf16[32,112,192]{2,1,0:T(8,128)(2,1)} %bitcast.14, bf16[192,768]{1,0:T(8,128)(2,1)} %refs_2_.1, bf16[768,192]{1,0:T(8,128)(2,1)} %copy.17.refs_3_), custom_call_target="tpu_custom_call" | custom-call | flops 8000000000 | bytes 6000000 | tf_op jit(solution)/shard_map/dense/pallas_call | solution.py:185
  202.7 0.0 copy-start.2
  202.7 2.3 pad_maximum_fusion
  205.0 5.7 %all-to-all-start.2 = ((bf16[32,48,192]{2,1,0:T(8,128)(2,1)}), bf16[32,48,192]{2,1,0:T(8,128)(2,1)S(1)}, u32[]{:S(2)}, u32[]{:S(2)}) async-start(bf16[32,48,192]{2,1,0:T(8,128)(2,1)} %pad_maximum_fusion), calls=%async_computation.2 | async-start | bytes 1572864 | tf_op jit(solution)/shard_map/all_to_all | solution.py:226
  210.7 0.0 copy-done.2
  210.7 2.5 %copy.18 = bf16[1,32,112,192]{2,3,1,0:T(8,128)(2,1)} copy(bf16[1,32,112,192]{3,2,1,0:T(8,128)(2,1)S(1)} %bitcast.13) | data formatting | bytes 2752512
  213.2 18.1 %all-to-all-done.2 = bf16[32,48,192]{2,1,0:T(8,128)(2,1)S(1)} async-done(((bf16[32,48,192]{2,1,0:T(8,128)(2,1)}), bf16[32,48,192]{2,1,0:T(8,128)(2,1)S(1)}, u32[]{:S(2)}, u32[]{:S(2)}) %all-to-all-start.2) | async-done | bytes 589856 | tf_op jit(solution)/shard_map/all_to_all | solution.py:226
  231.3 0.1 convert_reduce_fusion
  231.4 0.6 fusion
Async XLA Ops:
  68.5 5.0 %copy-start.4 = (bf16[192,576]{1,0:T(8,128)(2,1)S(1)}, bf16[192,576]{1,0:T(8,128)(2,1)}, u32[]{:S(2)}) copy-start(bf16[192,576]{1,0:T(8,128)(2,1)} %param.15) | copy-start | bytes 663556
  68.5 27.2 %all-to-all-start = ((bf16[4,28,32,192]{3,2,1,0:T(8,128)(2,1)}), bf16[4,28,32,192]{3,2,1,0:T(8,128)(2,1)S(1)}, u32[]{:S(2)}, u32[]{:S(2)}) async-start(bf16[4,28,32,192]{3,2,1,0:T(8,128)(2,1)} %bitcast.12), calls=%async_computation | async-start | bytes 3670016 | tf_op jit(solution)/shard_map/all_to_all | solution.py:215
  95.7 1.3 copy-start.1
  148.0 5.6 %copy-start.3 = (bf16[1,32,112,192]{2,3,1,0:T(8,128)(2,1)S(1)}, bf16[1,32,112,192]{2,3,1,0:T(8,128)(2,1)}, u32[]{:S(2)}) copy-start(bf16[1,32,112,192]{2,3,1,0:T(8,128)(2,1)} %param.19) | copy-start | bytes 4128772
  148.0 26.5 %all-to-all-start.1 = ((bf16[4,28,32,192]{3,2,1,0:T(8,128)(2,1)}), bf16[4,28,32,192]{3,2,1,0:T(8,128)(2,1)S(1)}, u32[]{:S(2)}, u32[]{:S(2)}) async-start(bf16[4,28,32,192]{3,2,1,0:T(8,128)(2,1)} %row.1), calls=%async_computation.1 | async-start | bytes 3670016 | tf_op jit(solution)/shard_map/all_to_all | solution.py:217
  174.5 1.3 copy-start
  202.7 8.0 %copy-start.2 = (bf16[32,112,192]{2,1,0:T(8,128)(2,1)S(1)}, bf16[32,112,192]{2,1,0:T(8,128)(2,1)}, u32[]{:S(2)}) copy-start(bf16[32,112,192]{2,1,0:T(8,128)(2,1)} %get-tuple-element.6) | copy-start | bytes 4128772
  205.0 26.3 %all-to-all-start.2 = ((bf16[32,48,192]{2,1,0:T(8,128)(2,1)}), bf16[32,48,192]{2,1,0:T(8,128)(2,1)S(1)}, u32[]{:S(2)}, u32[]{:S(2)}) async-start(bf16[32,48,192]{2,1,0:T(8,128)(2,1)} %pad_maximum_fusion), calls=%async_computation.2 | async-start | bytes 1572864 | tf_op jit(solution)/shard_map/all_to_all | solution.py:226

commit v2 on v1

v2 whole, which is shorter than its diff:
```python
import math

import jax
import jax.numpy as jnp
from jax import lax
from jax.experimental import pallas as pl
from jax.experimental.pallas import tpu as pltpu
from jax.sharding import PartitionSpec as P

HEADS = 6
HEAD_DIM = 32
NEG = -1e30
UNROLL = 8
GROUP = 4
LOG2E = math.log2(math.e)
SCALE = LOG2E / math.sqrt(HEAD_DIM)
AXES = ("tables", "cells")
F32 = jnp.float32
BF16 = jnp.bfloat16


def dot(a, b, ca, cb):
    return lax.dot_general(a, b, (((ca,), (cb,)), ((), ())), preferred_element_type=F32)


def layer_norm(values, axis):
    mean = jnp.mean(values, axis=axis, keepdims=True)
    centred = values - mean
    var = jnp.mean(centred * centred, axis=axis, keepdims=True)
    return centred * lax.rsqrt(var + 1e-05)


def attend(packs, limit):
    width, n = packs[0].shape[0] // 3, packs[0].shape[1]
    keep = lax.broadcasted_iota(jnp.int32, (n, 1), 0) < limit
    step = n if n <= 128 else 128
    jobs = [(i, h, q0) for i in range(len(packs)) for h in range(HEADS) for q0 in range(0, n, step)]
    scores, probs, outs = [], [], []
    for i, h, q0 in jobs:
        lo = h * HEAD_DIM
        keys = packs[i][width + lo : width + lo + HEAD_DIM]
        query = packs[i][lo : lo + HEAD_DIM, q0 : q0 + step]
        scores.append(dot(keys, query, 0, 0))
    for score in scores:
        score = jnp.where(keep, score, NEG)
        prob = jnp.exp2((score - jnp.max(score, axis=0, keepdims=True)) * SCALE)
        probs.append((prob.astype(BF16), 1.0 / jnp.sum(prob, axis=0, keepdims=True)))
    for (i, h, q0), (prob, inverse) in zip(jobs, probs):
        lo = 2 * width + h * HEAD_DIM
        outs.append((dot(packs[i][lo : lo + HEAD_DIM], prob, 1, 0), inverse))
    outs = [(out * inverse).astype(BF16) for out, inverse in outs]
    blocks = n // step
    result = []
    for i in range(len(packs)):
        heads = []
        for h in range(HEADS):
            at = (i * HEADS + h) * blocks
            cols = outs[at : at + blocks]
            heads.append(cols[0] if blocks == 1 else jnp.concatenate(cols, axis=1))
        result.append(jnp.concatenate(heads, axis=0))
    return result


def feature_kernel(limit_ref, x_ref, wn_ref, pn_ref, o_ref, lo_ref, hi_ref, w_ref, p_ref):
    rows, width, feats = x_ref.shape
    limit = limit_ref[0]

    @pl.when(pl.program_id(0) == 0)
    def _():
        w_ref[...] = wn_ref[...].T
        p_ref[...] = pn_ref[...].T

    unroll = UNROLL if rows % UNROLL == 0 else 1

    def body(i, carry):
        spots = [i * unroll + k for k in range(unroll)]
        cells = [x_ref[r] for r in spots]
        packs = [dot(w_ref[...], x, 1, 0).astype(BF16) for x in cells]
        attended = attend(packs, limit)
        mixed = [dot(p_ref[...], a, 1, 0) for a in attended]
        for r, x, m in zip(spots, cells, mixed):
            y = layer_norm(x.astype(F32) + m, 0)
            spot = pl.ds(r, feats, stride=rows)
            lo_ref[spot, :] = y[:128].T
            hi_ref[spot, :] = jnp.concatenate([y[128:], jnp.zeros((256 - width, feats), F32)], axis=0).T
        return carry

    lax.fori_loop(0, rows // unroll, body, 0)
    o_ref[:, :, :128] = lo_ref[...].reshape(feats, rows, 128).astype(BF16)
    o_ref[:, :, 128:] = hi_ref[...].reshape(feats, rows, 128)[:, :, : width - 128].astype(BF16)


def row_kernel(limit_ref, x_ref, wn_ref, p_ref, o_ref, w_ref):
    groups, block, rows, width = x_ref.shape
    limit = limit_ref[0]

    @pl.when(pl.program_id(0) == 0)
    def _():
        w_ref[...] = wn_ref[...].T


    unroll = block

    def body(i, carry):
        spots = [i * unroll + k for k in range(unroll)]
        cells = [x_ref[:, f].reshape(groups * rows, width) for f in spots]
        packs = [dot(w_ref[...], x, 1, 1).astype(BF16) for x in cells]
        attended = attend(packs, limit)
        mixed = [dot(a, p_ref[...], 0, 0) for a in attended]
        for f, x, m in zip(spots, cells, mixed):
            y = layer_norm(x.astype(F32) + m, -1)
            o_ref[:, f] = y.astype(BF16).reshape(groups, rows, width)
        return carry

    lax.fori_loop(0, block // unroll, body, 0)


def gelu_pair(x):
    bell = jnp.exp2(x * x * (-0.5 * LOG2E))
    t = 1.0 / (1.0 + (0.3275911 * math.sqrt(0.5)) * jnp.abs(x))
    poly = 0.5 * 1.061405429 * t + (0.5 * -1.453152027)
    poly = poly * t + (0.5 * 1.421413741)
    poly = poly * t + (0.5 * -0.284496736)
    poly = poly * t + (0.5 * 0.254829592)
    tail = poly * t * bell
    cdf = jnp.where(x < 0, tail, 1.0 - tail)
    return x * cdf, cdf + x * bell * (1.0 / math.sqrt(2.0 * math.pi))


def dense_kernel(factor, x_ref, c_ref, wi_ref, wo_ref, o_ref, gi_ref, go_ref, lo_ref, hi_ref, ai_ref, ao_ref):
    feats, rows, width = x_ref.shape
    cells = feats * rows
    step = pl.program_id(0)

    @pl.when(step == 0)
    def _():
        ai_ref[...] = jnp.zeros_like(ai_ref)
        ao_ref[...] = jnp.zeros_like(ao_ref)

    lo_ref[...] = x_ref[:, :, :128].astype(F32).reshape(cells, 128)
    hi_ref[:, : width - 128] = x_ref[:, :, 128:].astype(F32).reshape(cells, width - 128)
    group = GROUP if rows % GROUP == 0 else 1

    def body(i, carry):
        spots = [i * group + k for k in range(group)]
        parts, cots = [], []
        for r in spots:
            spot = pl.ds(r, feats, stride=rows)
            parts.append(jnp.concatenate([lo_ref[spot, :], hi_ref[spot, :][:, : width - 128]], axis=1).astype(BF16))
            cots.append(c_ref[r].T)
        normed = jnp.concatenate(parts, axis=0)
        cot = jnp.concatenate(cots, axis=0)
        act, slope = gelu_pair(dot(normed, wi_ref[...], 1, 0))
        act = act.astype(BF16)
        dpre = (dot(cot, wo_ref[...], 1, 0) * slope).astype(BF16)
        out = normed.astype(F32) + dot(act, wo_ref[...], 1, 1)
        for k, r in enumerate(spots):
            o_ref[r] = out[k * feats : (k + 1) * feats].T.astype(BF16)
        ai_ref[...] += dot(normed, dpre, 0, 0)
        ao_ref[...] += dot(cot, act, 0, 0)
        return carry

    lax.fori_loop(0, rows // group, body, 0)

    @pl.when(step == pl.num_programs(0) - 1)
    def _():
        gi_ref[...] = (ai_ref[...] * factor).T.astype(BF16)
        go_ref[...] = (ao_ref[...] * factor).T.astype(BF16)


def whole_spec(array):
    return pl.BlockSpec(array.shape, lambda i: (0,) * array.ndim)


def divisor(n, most):
    return max(k for k in range(1, most + 1) if n % k == 0)


def run_feature(limit, block, w_qkv, w_proj):
    rows, width, feats = block.shape
    part = 16 if rows % 16 == 0 else rows
    return pl.pallas_call(
        feature_kernel,
        grid=(rows // part,),
        out_shape=jax.ShapeDtypeStruct((feats, rows, width), BF16),
        in_specs=[
            pl.BlockSpec(memory_space=pltpu.SMEM),
            pl.BlockSpec((part, width, feats), lambda i: (i, 0, 0)),
            whole_spec(w_qkv),
            whole_spec(w_proj),
        ],
        out_specs=pl.BlockSpec((feats, part, width), lambda i: (0, i, 0)),
        scratch_shapes=[pltpu.VMEM((feats * part, 128), F32)] * 2
        + [pltpu.VMEM(w_qkv.shape[::-1], BF16), pltpu.VMEM(w_proj.shape[::-1], BF16)],
        cost_estimate=pl.CostEstimate(flops=4 * 10**9, bytes_accessed=4 * 10**6, transcendentals=0),
        name="feature",
    )(limit, block, w_qkv, w_proj)


def run_row(limit, columns, w_qkv, w_proj):
    groups, feats, rows, width = columns.shape
    part = divisor(feats, 7 if groups * rows <= 128 else 1)
    spec = pl.BlockSpec((groups, part, rows, width), lambda i: (0, i, 0, 0))
    return pl.pallas_call(
        row_kernel,
        grid=(feats // part,),
        out_shape=jax.ShapeDtypeStruct(columns.shape, BF16),
        in_specs=[pl.BlockSpec(memory_space=pltpu.SMEM), spec, whole_spec(w_qkv), whole_spec(w_proj)],
        out_specs=spec,
        scratch_shapes=[pltpu.VMEM(w_qkv.shape[::-1], BF16)],
        cost_estimate=pl.CostEstimate(flops=4 * 10**9, bytes_accessed=4 * 10**6, transcendentals=0),
        name="row",
    )(limit, columns, w_qkv, w_proj)


def run_dense(factor, normed, cot, w_in, w_out):
    feats, rows, width = normed.shape
    hidden = w_in.shape[1]
    part = 8 if rows % 8 == 0 else rows
    natural = pl.BlockSpec((part, width, feats), lambda i: (i, 0, 0))
    grad = pl.BlockSpec((hidden, width), lambda i: (0, 0))
    return pl.pallas_call(
        lambda *refs: dense_kernel(factor, *refs),
        grid=(rows // part,),
        out_shape=[
            jax.ShapeDtypeStruct((rows, width, feats), BF16),
            jax.ShapeDtypeStruct((hidden, width), BF16),
            jax.ShapeDtypeStruct((hidden, width), BF16),
        ],
        in_specs=[
            pl.BlockSpec((feats, part, width), lambda i: (0, i, 0)),
            natural,
            whole_spec(w_in),
            whole_spec(w_out),
        ],
        out_specs=[natural, grad, grad],
        scratch_shapes=[pltpu.VMEM((part * feats, 128), F32)] * 2 + [pltpu.VMEM((width, hidden), F32)] * 2,
        cost_estimate=pl.CostEstimate(flops=8 * 10**9, bytes_accessed=6 * 10**6, transcendentals=0),
        name="dense",
    )(normed, cot, w_in, w_out)


def per_device(
    cells_in, train_count, feat_count, feat_qkv, feat_proj, row_qkv, row_proj, w_in, w_out, cotangent
):
    block = cells_in[0]
    rows, feats, width = block.shape
    groups = lax.axis_size("cells")
    devices = groups * lax.axis_size("tables")
    mid = run_feature(feat_count, jnp.swapaxes(block, 1, 2), feat_qkv, feat_proj)
    columns = mid.reshape(groups, feats // groups, rows, width)
    columns = lax.all_to_all(columns, "cells", split_axis=0, concat_axis=0, tiled=True)
    done = run_row(train_count, columns, row_qkv, row_proj)
    normed = lax.all_to_all(done, "cells", split_axis=0, concat_axis=0, tiled=True)
    factor = 1.0 / math.sqrt(devices * rows * feats)
    output, part_in, part_out = run_dense(
        factor, normed.reshape(feats, rows, width), jnp.swapaxes(cotangent[0], 1, 2), w_in, w_out.T
    )
    own = part_in.shape[0] // devices
    sends = jnp.concatenate(
        [part_in.reshape(devices, own, width), part_out.reshape(devices, own, width)], axis=1
    )
    got = lax.all_to_all(sends, AXES, split_axis=0, concat_axis=0, tiled=True)
    total = jnp.sum(got.astype(F32), axis=0)
    return jnp.swapaxes(output, 1, 2)[None], total[:own].T, total[own:]


def solution(mesh):
    return jax.shard_map(
        per_device,
        mesh=mesh,
        in_specs=(
            P("tables", "cells", None, None),
            P("tables"),
            P("tables"),
            P(),
            P(),
            P(),
            P(),
            P(),
            P(),
            P("tables", "cells", None, None),
        ),
        out_specs=(
            P("tables", "cells", None, None),
            P(None, ("tables", "cells")),
            P(("tables", "cells"), None),
        ),
        check_vma=False,
    )
```

time: 233 us -> 126 us (0.54)
  Pallas kernels: 139 us -> 41 us
  blocking collectives: 0 us -> 53.4 us
  waiting for transfers between devices: 57.8 us -> 22.2 us
  local copies, waits for them, and re-layouts: 16.6 us -> 1.88 us
  starting transfers between devices: 13.8 us -> 4.23 us
    all_to_all x0 -> x2, blocking collectives: none -> 53.4 us  [the longest x1 27.3 us: per_device(): lax.all_to_all(done, 'cells', split_axis=0, concat_axis=0, tiled=True)]
    pallas_call x1, Pallas kernels: 61.6 us -> 12.9 us  [run_feature(): pl.pallas_call(feature_kernel, grid=(rows // part,), out_shape=jax.ShapeD...]
    pallas_call x1, Pallas kernels: 51 us -> 10.2 us  [run_row(): pl.pallas_call(row_kernel, grid=(feats // part,), out_shape=jax.ShapeDtyp...]
    all_to_all x2 -> x0, waiting for transfers between devices: 36.5 us -> none  [the longest x1 18.4 us: per_device(): lax.all_to_all(done, 'cells', split_axis=0, concat_axis=0, tiled=True)]
    unnamed x16 -> x2, local copies, waits for them, and re-layouts: 16 us -> 1.26 us
    all_to_all x2 -> x0, starting transfers between devices: 9.44 us -> none  [the longest x1 5.72 us: per_device(): got = lax.all_to_all(sends, AXES, split_axis=0, concat_axis=0, tiled=True)]
    pallas_call x1, Pallas kernels: 26.9 us -> 17.9 us  [run_dense(): pl.pallas_call(lambda *refs: dense_kernel(factor, *refs), grid=(rows // p...]
  transfers between devices with their start and end apart: 3 -> 1, of which waited for: 3 -> 1; matrix products, arithmetic and copies ran while one was open for 3% -> 0% of each run, Pallas kernels for 0% -> 0%
where the time goes in v2:
time: 126 us
  blocking collectives  53.4 us (42%)
  Pallas kernels  41 us (33%)
  waiting for transfers between devices  22.2 us (18%)
  starting transfers between devices  4.23 us (3%)
  between operations  1.94 us (2%)
  local copies, waits for them, and re-layouts  1.88 us (1%)
  other arithmetic  1.39 us (1%)
    all_to_all x1, blocking collectives, per_device(): lax.all_to_all(done, 'cells', split_axis=0, concat_axis=0, tiled=True)  27.3 us
    all_to_all x1, blocking collectives, per_device(): got = lax.all_to_all(sends, AXES, split_axis=0, concat_axis=0, tiled=True)  26.1 us
    all_to_all x1, waiting for transfers between devices, per_device(): lax.all_to_all(columns, 'cells', split_axis=0, concat_axis=0, tiled=True)  22.2 us
    pallas_call x1, Pallas kernels, run_dense(): pl.pallas_call(lambda *refs: dense_kernel(factor, *refs), grid=(rows // p...  17.9 us
    pallas_call x1, Pallas kernels, run_feature(): pl.pallas_call(feature_kernel, grid=(rows // part,), out_shape=jax.ShapeD...  12.9 us
    pallas_call x1, Pallas kernels, run_row(): pl.pallas_call(row_kernel, grid=(feats // part,), out_shape=jax.ShapeDtyp...  10.2 us
    all_to_all x1, starting transfers between devices, per_device(): lax.all_to_all(columns, 'cells', split_axis=0, concat_axis=0, tiled=True)  4.23 us
  transfers between devices with their start and end apart: 1, of which 1 were waited for; matrix products, arithmetic and copies ran while one was open for 0% of the time, Pallas kernels for 0%

profile of v2, /device:TPU:0, one launch (start us, length us, event | category | flops | bytes accessed | tf_op | source)
XLA Modules:
  0.0 126.0 jit_solution(7129989888100895818)
XLA Ops:
  1.3 12.9 %feature.1 = bf16[112,32,192]{2,1,0:T(8,128)(2,1)} custom-call(s32[1]{0:T(128)S(6)} %copy.14.limit_ref, bf16[32,192,112]{2,1,0:T(8,128)(2,1)} %bitcast.20, bf16[192,576]{1,0:T(8,128)(2,1)} %wn_ref.2, bf16[192,192]{1,0:T(8,128)(2,1)} %pn_ref.1), custom_call_target="tpu_custom_call" | custom-call | flops 4000000000 | bytes 4000000 | tf_op jit(solution)/shard_map/feature/pallas_call | solution.py:182
  14.2 4.2 %all-to-all-start = ((bf16[4,28,32,192]{3,2,1,0:T(8,128)(2,1)}), bf16[4,28,32,192]{3,2,1,0:T(8,128)(2,1)S(1)}, u32[]{:S(2)}, u32[]{:S(2)}) async-start(bf16[4,28,32,192]{3,2,1,0:T(8,128)(2,1)} %bitcast.16), calls=%async_computation | async-start | bytes 3670016 | tf_op jit(solution)/shard_map/all_to_all | solution.py:252
  19.1 22.2 %all-to-all-done.x_ref = bf16[4,28,32,192]{3,2,1,0:T(8,128)(2,1)S(1)} async-done(((bf16[4,28,32,192]{3,2,1,0:T(8,128)(2,1)}), bf16[4,28,32,192]{3,2,1,0:T(8,128)(2,1)S(1)}, u32[]{:S(2)}, u32[]{:S(2)}) %all-to-all-start) | async-done | bytes 1376288 | tf_op jit(solution)/shard_map/all_to_all | solution.py:252
  41.3 0.0 copy-start
  41.3 1.3 copy-done
  42.5 10.2 %row.1 = bf16[4,28,32,192]{3,2,1,0:T(8,128)(2,1)} custom-call(s32[1]{0:T(128)S(6)} %copy.13.limit_ref, bf16[4,28,32,192]{3,2,1,0:T(8,128)(2,1)} %copy-done, bf16[192,576]{1,0:T(8,128)(2,1)} %wn_ref.3, bf16[192,192]{1,0:T(8,128)(2,1)} %p_ref.1), custom_call_target="tpu_custom_call" | custom-call | flops 4000000000 | bytes 4000000 | tf_op jit(solution)/shard_map/row/pallas_call | solution.py:204
  52.7 27.3 %all_to_all.15 = bf16[4,28,32,192]{3,2,1,0:T(8,128)(2,1)} all-to-all(bf16[4,28,32,192]{3,2,1,0:T(8,128)(2,1)} %row.1), channel_id=1, replica_groups=mesh['tables'=8,'cells'=4] {'cells'}, dimensions={0} | all-to-all | bytes 2752512 | tf_op jit(solution)/shard_map/all_to_all | solution.py:254
  80.0 17.9 %dense.1 = (bf16[32,192,112]{2,1,0:T(8,128)(2,1)}, bf16[768,192]{1,0:T(8,128)(2,1)}, bf16[768,192]{1,0:T(8,128)(2,1)}) custom-call(bf16[112,32,192]{2,1,0:T(8,128)(2,1)} %bitcast.17, bf16[32,192,112]{2,1,0:T(8,128)(2,1)} %bitcast.21, bf16[192,768]{1,0:T(8,128)(2,1)} %refs_2_.1, bf16[192,768]{1,0:T(8,128)(2,1)} %bitcast.22), custom_call_target="tpu_custom_call" | custom-call | flops 8000000000 | bytes 6000000 | tf_op jit(solution)/shard_map/dense/pallas_call | solution.py:222
  97.9 1.3 pad_maximum_fusion
  99.2 26.1 %all_to_all.16 = bf16[32,48,192]{2,1,0:T(8,128)(2,1)S(1)} all-to-all(bf16[32,48,192]{2,1,0:T(8,128)(2,1)S(1)} %pad_maximum_fusion), channel_id=1, replica_groups=mesh['tables'=8,'cells'=4] {'tables','cells'}, dimensions={0} | all-to-all | bytes 1179648 | tf_op jit(solution)/shard_map/all_to_all | solution.py:263
  125.3 0.1 convert_reduce_fusion
  125.4 0.6 fusion
Async XLA Ops:
  14.2 27.1 %all-to-all-start = ((bf16[4,28,32,192]{3,2,1,0:T(8,128)(2,1)}), bf16[4,28,32,192]{3,2,1,0:T(8,128)(2,1)S(1)}, u32[]{:S(2)}, u32[]{:S(2)}) async-start(bf16[4,28,32,192]{3,2,1,0:T(8,128)(2,1)} %bitcast.16), calls=%async_computation | async-start | bytes 3670016 | tf_op jit(solution)/shard_map/all_to_all | solution.py:252
  41.3 1.3 copy-start

commit v3 on v2

--- a/solution.py
+++ b/solution.py
@@ -240,6 +240,73 @@
     )(normed, cot, w_in, w_out)
 
 
+def exchange_kernel(axes, sizes, x_ref, o_ref, own_ref, own_sem, send_sem, recv_sem):
+    count = math.prod(sizes)
+    me = 0
+    for axis, size in zip(axes, sizes):
+        me = me * size + lax.axis_index(axis)
+
+    def target(k):
+        peer = lax.rem(me + k, count)
+        if len(axes) == 1:
+            return peer, {axes[0]: peer}
+        return peer, {axes[0]: lax.div(peer, sizes[1]), axes[1]: lax.rem(peer, sizes[1])}
+
+    def copy(k):
+        peer, device = target(k)
+        return pltpu.make_async_remote_copy(
+            src_ref=x_ref.at[peer],
+            dst_ref=o_ref.at[me],
+            send_sem=send_sem.at[k],
+            recv_sem=recv_sem.at[k],
+            device_id=device,
+            device_id_type=pl.DeviceIdType.MESH,
+        )
+
+    barrier = pltpu.get_barrier_semaphore()
+
+    def greet(k, carry):
+        pl.semaphore_signal(barrier, inc=1, device_id=target(k)[1], device_id_type=pl.DeviceIdType.MESH)
+        return carry
+
+    def start(k, carry):
+        copy(k).start()
+        return carry
+
+    def finish(k, carry):
+        copy(k).wait()
+        return carry
+
+    load = pltpu.make_async_copy(x_ref.at[me], own_ref, own_sem.at[0])
+    load.start()
+    lax.fori_loop(1, count, greet, 0)
+    pl.semaphore_wait(barrier, count - 1)
+    lax.fori_loop(1, count, start, 0)
+    load.wait()
+    store = pltpu.make_async_copy(own_ref, o_ref.at[me], own_sem.at[1])
+    store.start()
+    lax.fori_loop(1, count, finish, 0)
+    store.wait()
+
+
+def exchange(array, axes, ident):
+    sizes = [lax.axis_size(axis) for axis in axes]
+    return pl.pallas_call(
+        lambda *refs: exchange_kernel(axes, sizes, *refs),
+        out_shape=jax.ShapeDtypeStruct(array.shape, array.dtype),
+        in_specs=[pl.BlockSpec(memory_space=pl.ANY)],
+        out_specs=pl.BlockSpec(memory_space=pl.ANY),
+        scratch_shapes=[
+            pltpu.VMEM(array.shape[1:], array.dtype),
+            pltpu.SemaphoreType.DMA((2,)),
+            pltpu.SemaphoreType.DMA((array.shape[0],)),
+            pltpu.SemaphoreType.DMA((array.shape[0],)),
+        ],
+        compiler_params=pltpu.CompilerParams(collective_id=ident, has_side_effects=True),
+        name="exchange%d" % ident,
+    )(array)
+
+
 def per_device(
     cells_in, train_count, feat_count, feat_qkv, feat_proj, row_qkv, row_proj, w_in, w_out, cotangent
 ):
@@ -249,9 +316,9 @@
     devices = groups * lax.axis_size("tables")
     mid = run_feature(feat_count, jnp.swapaxes(block, 1, 2), feat_qkv, feat_proj)
     columns = mid.reshape(groups, feats // groups, rows, width)
-    columns = lax.all_to_all(columns, "cells", split_axis=0, concat_axis=0, tiled=True)
+    columns = exchange(columns, ("cells",), 0)
     done = run_row(train_count, columns, row_qkv, row_proj)
-    normed = lax.all_to_all(done, "cells", split_axis=0, concat_axis=0, tiled=True)
+    normed = exchange(done, ("cells",), 1)
     factor = 1.0 / math.sqrt(devices * rows * feats)
     output, part_in, part_out = run_dense(
         factor, normed.reshape(feats, rows, width), jnp.swapaxes(cotangent[0], 1, 2), w_in, w_out.T
@@ -260,7 +327,7 @@
     sends = jnp.concatenate(
         [part_in.reshape(devices, own, width), part_out.reshape(devices, own, width)], axis=1
     )
-    got = lax.all_to_all(sends, AXES, split_axis=0, concat_axis=0, tiled=True)
+    got = exchange(sends, AXES, 2)
     total = jnp.sum(got.astype(F32), axis=0)
     return jnp.swapaxes(output, 1, 2)[None], total[:own].T, total[own:]
 

time: 126 us -> 116 us (0.921)
  the two profiles are of different devices: /device:TPU:0 before, /device:TPU:15 now
where the time goes in v3:
time: 116 us
  Pallas kernels  110 us (95%)
  other arithmetic  3.41 us (3%)
  between operations  1.95 us (2%)
    pallas_call x3, Pallas kernels, exchange(): pl.pallas_call(lambda *refs: exchange_kernel(axes, sizes, *refs), out_sha...  68.9 us
    pallas_call x1, Pallas kernels, run_dense(): pl.pallas_call(lambda *refs: dense_kernel(factor, *refs), grid=(rows // p...  18 us
    pallas_call x1, Pallas kernels, run_feature(): pl.pallas_call(feature_kernel, grid=(rows // part,), out_shape=jax.ShapeD...  12.9 us
    pallas_call x1, Pallas kernels, run_row(): pl.pallas_call(row_kernel, grid=(feats // part,), out_shape=jax.ShapeDtyp...  10.2 us

profile of v3, /device:TPU:15, one launch (start us, length us, event | category | flops | bytes accessed | tf_op | source)
XLA Modules:
  0.0 115.9 jit_solution(6310029254567360137)
XLA Ops:
  1.9 12.9 %feature.1 = bf16[112,32,192]{2,1,0:T(8,128)(2,1)} custom-call(s32[1]{0:T(128)S(6)} %copy.14.limit_ref, bf16[32,192,112]{2,1,0:T(8,128)(2,1)} %bitcast.20, bf16[192,576]{1,0:T(8,128)(2,1)} %wn_ref.2, bf16[192,192]{1,0:T(8,128)(2,1)} %pn_ref.1), custom_call_target="tpu_custom_call" | custom-call | flops 4000000000 | bytes 4000000 | tf_op jit(solution)/shard_map/feature/pallas_call | solution.py:182
  14.8 23.0 %exchange0.1.x_ref = bf16[4,28,32,192]{3,2,1,0:T(8,128)(2,1)} custom-call(bf16[4,28,32,192]{3,2,1,0:T(8,128)(2,1)} %bitcast.17), custom_call_target="tpu_custom_call" | custom-call | tf_op jit(solution)/shard_map/exchange0/pallas_call | solution.py:294
  37.9 10.2 %row.1.refs_0_ = bf16[4,28,32,192]{3,2,1,0:T(8,128)(2,1)} custom-call(s32[1]{0:T(128)S(6)} %copy.13.limit_ref, bf16[4,28,32,192]{3,2,1,0:T(8,128)(2,1)} %exchange0.1.x_ref, bf16[192,576]{1,0:T(8,128)(2,1)} %wn_ref.3, bf16[192,192]{1,0:T(8,128)(2,1)} %p_ref.1), custom_call_target="tpu_custom_call" | custom-call | flops 4000000000 | bytes 4000000 | tf_op jit(solution)/shard_map/row/pallas_call | solution.py:204
  48.1 22.5 %exchange1.1 = bf16[4,28,32,192]{3,2,1,0:T(8,128)(2,1)} custom-call(bf16[4,28,32,192]{3,2,1,0:T(8,128)(2,1)} %row.1.refs_0_), custom_call_target="tpu_custom_call" | custom-call | tf_op jit(solution)/shard_map/exchange1/pallas_call | solution.py:294
  70.5 18.0 %dense.1 = (bf16[32,192,112]{2,1,0:T(8,128)(2,1)}, bf16[768,192]{1,0:T(8,128)(2,1)}, bf16[768,192]{1,0:T(8,128)(2,1)}) custom-call(bf16[112,32,192]{2,1,0:T(8,128)(2,1)} %bitcast.16, bf16[32,192,112]{2,1,0:T(8,128)(2,1)} %bitcast.21, bf16[192,768]{1,0:T(8,128)(2,1)} %refs_2_.1, bf16[192,768]{1,0:T(8,128)(2,1)} %bitcast.22), custom_call_target="tpu_custom_call" | custom-call | flops 8000000000 | bytes 6000000 | tf_op jit(solution)/shard_map/dense/pallas_call | solution.py:222
  88.5 2.1 %pad_maximum_fusion.refs_0_ = bf16[32,48,192]{2,1,0:T(8,128)(2,1)} fusion(bf16[32,24,192]{2,1,0:T(8,128)(2,1)} %bitcast.19, bf16[32,24,192]{2,1,0:T(8,128)(2,1)} %bitcast.18), kind=kLoop, calls=%fused_computation.1 | loop fusion | flops 1179648 | bytes 1179648 | tf_op jit(solution)/shard_map/concatenate | solution.py:327
  90.6 23.4 %exchange2.1 = bf16[32,48,192]{2,1,0:T(8,128)(2,1)} custom-call(bf16[32,48,192]{2,1,0:T(8,128)(2,1)} %pad_maximum_fusion.refs_0_), custom_call_target="tpu_custom_call" | custom-call | tf_op jit(solution)/shard_map/exchange2/pallas_call | solution.py:294
  114.0 1.3 %convert_reduce_fusion = f32[48,192]{1,0:T(8,128)S(1)} fusion(bf16[32,48,192]{2,1,0:T(8,128)(2,1)} %exchange2.1), kind=kLoop, calls=%fused_computation | loop fusion | flops 580608 | bytes 626688 | tf_op jit(solution)/shard_map/reduce_sum | solution.py:331
  115.3 0.6 fusion
